TPU v7x, 32 devices: a whole 2x2x4 slice. The times are simulated.
32 devices in a mesh: seq: 4 (over y, x), head: 8 (over z, core).
Axes of the slice: x: 2, y: 2, z: 4, core: 2. Of those that a mesh axis runs over, the one named last changes fastest.
Arguments:
- queries: bfloat16 [8192, 4096], P(('seq', 'head')), may hold values from -6 to 6
- key_vectors: bfloat16 [8192, 4096], P(('seq', 'head')), may hold values from -0.375 to 0.375
- values: bfloat16 [8192, 8192], P(('seq', 'head')), may hold values from -6 to 6
- decay_log: bfloat16 [8192, 16], P(('seq', 'head')), may hold values from -0.8 to 0, as said below
- gate_input: bfloat16 [8192, 8192], P(('seq', 'head')), may hold values from -6 to 6
Outputs:
- retention_out: bfloat16 [8192, 8192], P(('seq', 'head'))
Inputs may be any that keep to these rules, and one draw needn't show every extreme that they name: `decay_log`: every entry is negative.
All inputs are finite; a program needn't handle non-finite values.
Results may differ from a plain program's by a relative error of at most 0.0063.
Values may be sent and summed in bfloat16 or wider, within the bound.
A program may use at most 128 MiB of HBM per device.

v0:
```python
import jax
import jax.numpy as jnp
from jax import lax
from jax.sharding import PartitionSpec as P

BLOCK = 512


def carried_in(part, axis, combine, identity):
    place = lax.axis_index(axis)
    gathered = jax.tree.map(lambda a: lax.all_gather(a, axis), part)
    state = jax.tree.map(lambda a, e: jnp.zeros_like(a) + jnp.asarray(e, a.dtype), part, identity)

    def one(lap, state):
        return combine(
            state, jax.tree.map(lambda a: lax.dynamic_index_in_dim(a, lap, 0, False), gathered)
        )

    return lax.fori_loop(0, place, one, state)


def as_sent(shard):
    return jax.tree.map(lambda a: a.astype(jnp.bfloat16) if a.dtype == jnp.float32 else a, shard)


def partner(value, axis, apart):
    mask = 2**apart
    pairs = [(source, source ^ mask) for source in range(lax.axis_size(axis))]
    return lax.ppermute(value, axis, pairs)


def combine_states(earlier, later):
    return (earlier[0] * later[0], later[0][:, None, None] * earlier[1] + later[1])


def prefix_state(damping, closing):
    identity = (jnp.ones_like(damping), jnp.zeros_like(closing))
    scanned = carried_in((damping, closing), "seq", combine_states, identity)
    incoming = scanned[1]
    return incoming


def retain_items(query_part, key_part, value_part, decay_part, carry_in):
    length, count, key_width = query_part.shape
    width = value_part.shape[2]
    blocks = length // BLOCK
    running = jnp.cumsum(decay_part.astype(jnp.float32).reshape(blocks, BLOCK, count), axis=1)
    block_decay = running[:, -1, :]
    query_blocks = query_part.reshape(blocks, BLOCK, count, key_width)
    key_blocks = key_part.reshape(blocks, BLOCK, count, key_width)
    value_blocks = value_part.reshape(blocks, BLOCK, count, width)
    faded = (
        key_blocks.astype(jnp.float32) * jnp.exp(block_decay[:, None, :] - running)[..., None]
    ).astype(jnp.bfloat16)
    additions = jnp.einsum(
        "bjnd,bjnw->bndw", faded, value_blocks, preferred_element_type=jnp.float32
    )

    def advance(carried_state, pieces):
        rate_row, addition = pieces
        return (jnp.exp(rate_row)[:, None, None] * carried_state + addition, carried_state)

    initial = jnp.zeros((count, key_width, width), jnp.float32)
    closing, local_starts = lax.scan(advance, initial, (block_decay, additions))
    damping = jnp.exp(jnp.sum(block_decay, axis=0))
    incoming = carry_in(damping, closing)
    before = jnp.cumsum(block_decay, axis=0) - block_decay
    starts = local_starts + jnp.exp(before)[:, :, None, None] * incoming[None]
    causal = jnp.arange(BLOCK)[:, None] >= jnp.arange(BLOCK)[None, :]

    def emit_block(pieces):
        query_block, key_block, value_block, running_block, start_state = pieces
        scores = jnp.einsum(
            "ind,jnd->nij", query_block, key_block, preferred_element_type=jnp.float32
        )
        spread = running_block.T[:, :, None] - running_block.T[:, None, :]
        factor = jnp.exp(jnp.where(causal[None], spread, -jnp.inf))
        weights = (scores * factor).astype(jnp.bfloat16)
        within = jnp.einsum(
            "nij,jnw->inw", weights, value_block, preferred_element_type=jnp.float32
        )
        across = jnp.einsum(
            "ind,ndw->inw",
            query_block,
            start_state.astype(jnp.bfloat16),
            preferred_element_type=jnp.float32,
        )
        across = across * jnp.exp(running_block)[:, :, None]
        return (within + across).astype(jnp.bfloat16)

    retained = lax.map(emit_block, (query_blocks, key_blocks, value_blocks, running, starts))
    return retained.reshape(length, count, width)


def send_back(retained):
    return lax.all_to_all(retained[:, None], "head", split_axis=0, concat_axis=1, tiled=True)


def regroup_by_heads(queries, key_vectors, values, decay_log):
    rows_here = queries.shape[0]
    head_count = decay_log.shape[1]
    key_width = queries.shape[1] // head_count
    value_width = values.shape[1] // head_count
    groups = lax.axis_size("head")
    if groups > head_count:
        half = groups // 2
        bit = half.bit_length() - 1
        upper = lax.axis_index("head") >= half
        cut = rows_here // 2
        inputs = (queries, key_vectors, values, decay_log)
        firsts = tuple((item[:cut] for item in inputs))
        seconds = tuple((item[cut:] for item in inputs))
        outgoing = tuple((jnp.where(upper, one, two) for one, two in zip(firsts, seconds)))
        arrived = jax.tree.map(
            lambda part, own: part.astype(own.dtype),
            partner(as_sent(outgoing), "head", bit),
            outgoing,
        )
        part_zero = tuple((jnp.where(upper, got, one) for got, one in zip(arrived, firsts)))
        part_one = tuple((jnp.where(upper, two, got) for got, two in zip(arrived, seconds)))
        sending = tuple(
            (
                jnp.stack((one, two), axis=1).reshape(cut, groups, 1, -1)
                for one, two in zip(part_zero, part_one)
            )
        )
        per_here = 1

        def carry_in(damping, closing):
            other_damping, other_closing = partner((damping, closing), "head", bit)
            lower_damping = jnp.where(upper, other_damping, damping)
            lower_closing = jnp.where(upper, other_closing, closing)
            higher_damping = jnp.where(upper, damping, other_damping)
            higher_closing = jnp.where(upper, closing, other_closing)
            group_damping, group_closing = combine_states(
                (lower_damping, lower_closing), (higher_damping, higher_closing)
            )
            group_in = prefix_state(group_damping, group_closing)
            shifted = lower_damping[:, None, None] * group_in + lower_closing
            return jnp.where(upper, shifted, group_in)

    else:
        per_here = head_count // groups
        sending = (
            queries.reshape(rows_here, groups, per_here, key_width),
            key_vectors.reshape(rows_here, groups, per_here, key_width),
            values.reshape(rows_here, groups, per_here, value_width),
            decay_log.reshape(rows_here, groups, per_here, 1),
        )
        carry_in = prefix_state
    received = jax.tree.map(
        lambda part, own: part.astype(own.dtype),
        lax.all_to_all(as_sent(sending), "head", split_axis=1, concat_axis=0, tiled=True),
        sending,
    )
    received = tuple((item[:, 0] for item in received))
    length = received[0].shape[0]
    if groups > head_count:
        received = tuple(
            (
                item.reshape(2, half, cut, per_here, item.shape[-1])
                .swapaxes(0, 1)
                .reshape(length, per_here, item.shape[-1])
                for item in received
            )
        )
    query_got, key_got, value_got, decay_got = received
    retained = retain_items(query_got, key_got, value_got, decay_got[:, :, 0], carry_in)
    if groups > head_count:
        retained = (
            retained.reshape(half, 2, cut, per_here, value_width)
            .swapaxes(0, 1)
            .reshape(length, per_here, value_width)
        )
    returned = send_back(retained)
    if groups > head_count:
        returned = returned.reshape(cut, 2, head_count * value_width)
        first_out = returned[:, 0]
        second_out = returned[:, 1]
        leaving = jnp.where(upper, first_out, second_out)
        came_back = partner(as_sent(leaving), "head", bit).astype(leaving.dtype)
        returned = jnp.concatenate(
            (jnp.where(upper, came_back, first_out), jnp.where(upper, second_out, came_back)),
            axis=0,
        )
    return returned


def shards(queries, key_vectors, values, decay_log, gate_input):
    rows_here = queries.shape[0]
    head_count = decay_log.shape[1]
    value_width = values.shape[1] // head_count
    gathered_out = regroup_by_heads(queries, key_vectors, values, decay_log)
    retained_all = gathered_out.reshape(rows_here, head_count, value_width).astype(jnp.float32)
    average = jnp.mean(retained_all, axis=2, keepdims=True)
    centered = retained_all - average
    variance = jnp.mean(centered * centered, axis=2, keepdims=True)
    normed = centered / jnp.sqrt(variance + 1e-06)
    gated = (
        jax.nn.silu(gate_input.astype(jnp.float32).reshape(rows_here, head_count, value_width))
        * normed
    )
    return gated.astype(jnp.bfloat16).reshape(rows_here, head_count * value_width)


def solution(mesh):
    in_specs = (
        P(("seq", "head"), None),
        P(("seq", "head"), None),
        P(("seq", "head"), None),
        P(("seq", "head"), None),
        P(("seq", "head"), None),
    )
    out_specs = P(("seq", "head"), None)
    return jax.shard_map(shards, mesh=mesh, in_specs=in_specs, out_specs=out_specs, check_vma=False)
```

profile of v0, /device:TPU:0, one launch (start us, length us, event | category | flops | bytes accessed | tf_op | source)
XLA Modules:
  0.0 438.3 jit_solution(11047926079383961663)
XLA Ops:
  6.5 1.3 reshape.124
  7.8 6.4 %all-to-all-start.3 = ((bf16[256,8,2,1]{0,2,3,1:T(2,128)(2,1)}), bf16[256,8,2,1]{0,2,3,1:T(2,128)(2,1)S(1)}, u32[]{:S(2)}, u32[]{:S(2)}) async-start(bf16[256,8,2,1]{0,2,3,1:T(2,128)(2,1)} %reshape.124), calls=%async_computation.3 | async-start | bytes 16384 | tf_op jit(solution)/shard_map/all_to_all | solution.py:153
  14.2 4.1 copy.95
  18.3 1.5 all-to-all-done.3
  19.8 3.6 all-to-all-start.2
  23.4 6.4 %copy.91 = bf16[256,8192]{0,1:T(8,128)(2,1)} copy(bf16[256,8192]{1,0:T(8,128)(2,1)} %param.13) | data formatting | bytes 8388608 | tf_op args[2]
  29.8 42.6 %all-to-all-done.2 = bf16[256,8,2,256]{0,3,2,1:T(8,128)(2,1)S(1)} async-done(((bf16[256,8,2,256]{0,3,2,1:T(8,128)(2,1)}), bf16[256,8,2,256]{0,3,2,1:T(8,128)(2,1)S(1)}, u32[]{:S(2)}, u32[]{:S(2)}) %all-to-all-start.2) | async-done | bytes 2097184 | tf_op jit(solution)/shard_map/all_to_all | solution.py:153
  72.4 4.6 %all-to-all-start = ((bf16[256,8,2,512]{0,3,2,1:T(8,128)(2,1)}), bf16[256,8,2,512]{0,3,2,1:T(8,128)(2,1)}, u32[]{:S(2)}, u32[]{:S(2)}) async-start(bf16[256,8,2,512]{0,3,2,1:T(8,128)(2,1)} %bitcast.144), calls=%async_computation | async-start | bytes 8388608 | tf_op jit(solution)/shard_map/all_to_all | solution.py:153
  77.1 2.4 reduce-window.6
  81.0 2.4 copy.96
  83.4 87.6 %all-to-all-done = bf16[256,8,2,512]{0,3,2,1:T(8,128)(2,1)} async-done(((bf16[256,8,2,512]{0,3,2,1:T(8,128)(2,1)}), bf16[256,8,2,512]{0,3,2,1:T(8,128)(2,1)}, u32[]{:S(2)}, u32[]{:S(2)}) %all-to-all-start) | async-done | bytes 4194336 | tf_op jit(solution)/shard_map/all_to_all | solution.py:153
  171.0 6.4 %copy.92 = bf16[8,256,1,2,512]{4,1,0,3,2:T(8,128)(2,1)} copy(bf16[8,256,1,2,512]{1,4,3,0,2:T(8,128)(2,1)} %bitcast.4) | data formatting | bytes 8388608 | tf_op jit(solution)/shard_map/all_to_all | solution.py:153
  177.3 5.8 %fusion.36 = f32[4,2,256,512]{3,2,1,0:T(8,128)} fusion(bf16[4,512,2,512]{3,1,0,2:T(8,128)(2,1)} %bitcast.151, bf16[4,512,2,256]{3,1,0,2:T(8,128)(2,1)S(1)} %bitcast.155, f32[4,512,2]{1,0,2:T(4,128)S(1)} %copy.99), kind=kOutput, calls=%fused_computation.48 | convolution fusion | flops 1076887552 | bytes 10502144 | tf_op jit(solution)/shard_map/bjnd,bjnw->bndw/dot_general | solution.py:55
  183.2 10.5 %while.38 = (s32[]{:T(128)}, f32[2,256,512]{2,1,0:T(8,128)S(1)}, f32[4,2,256,512]{3,2,1,0:T(8,128)}, f32[4,2]{1,0:T(4,128)S(1)}, f32[4,2,256,512]{3,2,1,0:T(8,128)}, /*index=5*/s32[]{:T(128)}, s32[]{:T(128)}) while((s32[]{:T(128)}, f32[2,256,512]{2,1,0:T(8,128)S(1)}, f32[4,2,256,512]{3,2,1,0:T(8,128)}, f32[4,2]{1,0:T(4,128)S(1)}, ...), condition=%wide.region_3.4_spmd.clone, body=%wide.region_2.3_spmd.clone.sunk | while | flops 1048579 | bytes 5243512 | solution.py:64
  183.2 1.2 bitcast_dynamic-update-slice_fusion.2
  184.4 1.5 bitcast_add_fusion.5
  187.0 1.5 bitcast_add_fusion.5
  188.5 1.1 bitcast_dynamic-update-slice_fusion.2
  189.6 1.5 bitcast_add_fusion.5
  192.2 1.5 bitcast_add_fusion.5
  194.8 2.5 copy.93
  197.3 3.6 all-to-all-start.1
  202.4 10.4 %all-reduce = f32[8]{0:T(128)S(1)} all-reduce(f32[8]{0:T(128)S(1)} %exponential_dynamic-update-slice_fusion), channel_id=2, replica_groups=mesh['seq'=4,'head'=8] {'seq'}, use_global_device_ids=true, to_apply=%add | all-reduce | flops 8 | bytes 64
  213.1 36.7 %all-to-all-done.1 = bf16[256,8,2,256]{0,3,2,1:T(8,128)(2,1)S(1)} async-done(((bf16[256,8,2,256]{0,3,2,1:T(8,128)(2,1)}), bf16[256,8,2,256]{0,3,2,1:T(8,128)(2,1)S(1)}, u32[]{:S(2)}, u32[]{:S(2)}) %all-to-all-start.1) | async-done | bytes 2097184 | tf_op jit(solution)/shard_map/all_to_all | solution.py:153
  249.8 2.4 copy.94
  252.4 4.3 multiply_add_fusion
  256.7 33.7 %while.37 = (s32[]{:T(128)}, bf16[4,512,2,512]{3,1,0,2:T(8,128)(2,1)}, bf16[4,512,2,512]{3,1,0,2:T(8,128)(2,1)}, bf16[4,512,2,256]{3,1,0,2:T(8,128)(2,1)}, bf16[...) while((s32[]{:T(128)}, ...), condition=%wide.region_9.10_spmd.clone, body=%wide.region_8.9_spmd.clone.sunk | while | flops 1077673984 | bytes 15235681 | solution.py:91
  256.8 2.9 fusion.53
  259.7 1.1 constant_dynamic-slice_fusion.3
  261.8 1.7 fusion.54
  265.2 2.9 fusion.53
  268.1 1.1 constant_dynamic-slice_fusion.3
  270.2 1.7 fusion.54
  273.6 2.9 fusion.53
  276.6 1.1 constant_dynamic-slice_fusion.3
  278.7 1.7 fusion.54
  282.0 2.9 fusion.53
  285.0 1.1 constant_dynamic-slice_fusion.3
  287.1 1.7 fusion.54
  290.4 10.1 %copy.109 = bf16[2048,1,2,512]{3,2,1,0:T(2,128)(2,1)} copy(bf16[2048,1,2,512]{3,0,2,1:T(8,128)(2,1)} %bitcast.153) | data formatting | bytes 8388608 | tf_op jit(solution)/shard_map/broadcast_in_dim;reshape | solution.py:96
  300.5 4.8 %all-to-all-start.4 = ((bf16[2048,1,2,512]{3,2,1,0:T(2,128)(2,1)}), bf16[2048,1,2,512]{3,2,1,0:T(2,128)(2,1)}, u32[]{:S(2)}, u32[]{:S(2)}) async-start(bf16[2048,1,2,512]{3,2,1,0:T(2,128)(2,1)} %copy.109), calls=%async_computation.4 | async-start | bytes 8388608 | tf_op jit(solution)/shard_map/all_to_all | solution.py:96
  305.2 6.4 %copy.90 = bf16[256,8192]{0,1:T(8,128)(2,1)} copy(bf16[256,8192]{1,0:T(8,128)(2,1)} %param.15) | data formatting | bytes 8388608 | tf_op args[4]
  311.6 87.4 %all-to-all-done.4 = bf16[2048,1,2,512]{3,2,1,0:T(2,128)(2,1)} async-done(((bf16[2048,1,2,512]{3,2,1,0:T(2,128)(2,1)}), bf16[2048,1,2,512]{3,2,1,0:T(2,128)(2,1)}, u32[]{:S(2)}, u32[]{:S(2)}) %all-to-all-start.4) | async-done | bytes 4194336 | tf_op jit(solution)/shard_map/all_to_all | solution.py:96
  399.0 7.1 %fusion.39 = (bf16[2048,1,2,512]{3,0,2,1:T(8,128)(2,1)S(1)}, f32[256,8,1,2,512]{4,0,1,3,2:T(8,128)}) fusion(bf16[2048,1,2,512]{3,2,1,0:T(2,128)(2,1)} %all-to-all-done.4), kind=kLoop, calls=%fused_computation.62 | loop fusion | flops 2097152 | bytes 16777216 | tf_op jit(solution)/shard_map/all_to_all | solution.py:96
  406.8 1.7 multiply_reduce_fusion
  408.6 9.1 %copy.111 = f32[256,8,1,2,512]{0,4,3,1,2:T(8,128)} copy(f32[256,8,1,2,512]{4,0,1,3,2:T(8,128)} %get-tuple-element.264) | data formatting | bytes 16777216 | tf_op jit(solution)/shard_map/convert_element_type | solution.py:194
  417.8 7.3 %fusion.34 = bf16[256,8192]{0,1:T(8,128)(2,1)} fusion(f32[256,8,1,2,512]{0,4,3,1,2:T(8,128)} %copy.111, bf16[256,8192]{0,1:T(8,128)(2,1)} %copy.90, f32[256,16]{0,1:T(8,128)S(1)} %sqrt.12, f32[256,16]{0,1:T(8,128)S(1)} %div.26), kind=kLoop, calls=%fused_computation.46 | loop fusion | flops 18874368 | bytes 16809984 | tf_op jit(solution)/shard_map/convert_element_type | solution.py:203
  425.1 6.3 %copy.114 = bf16[256,8192]{1,0:T(8,128)(2,1)} copy(bf16[256,8192]{0,1:T(8,128)(2,1)} %fusion.34) | data formatting | bytes 8388608 | tf_op jit(solution)/shard_map/convert_element_type | solution.py:203
  (71 shorter events, 17.5 us)
Async XLA Ops:
  7.8 12.0 %all-to-all-start.3 = ((bf16[256,8,2,1]{0,2,3,1:T(2,128)(2,1)}), bf16[256,8,2,1]{0,2,3,1:T(2,128)(2,1)S(1)}, u32[]{:S(2)}, u32[]{:S(2)}) async-start(bf16[256,8,2,1]{0,2,3,1:T(2,128)(2,1)} %reshape.124), calls=%async_computation.3 | async-start | bytes 16384 | tf_op jit(solution)/shard_map/all_to_all | solution.py:153
  19.8 52.6 %all-to-all-start.2 = ((bf16[256,8,2,256]{0,3,2,1:T(8,128)(2,1)}), bf16[256,8,2,256]{0,3,2,1:T(8,128)(2,1)S(1)}, u32[]{:S(2)}, u32[]{:S(2)}) async-start(bf16[256,8,2,256]{0,3,2,1:T(8,128)(2,1)} %bitcast.149), calls=%async_computation.2 | async-start | bytes 4194304 | tf_op jit(solution)/shard_map/all_to_all | solution.py:153
  72.4 98.5 %all-to-all-start = ((bf16[256,8,2,512]{0,3,2,1:T(8,128)(2,1)}), bf16[256,8,2,512]{0,3,2,1:T(8,128)(2,1)}, u32[]{:S(2)}, u32[]{:S(2)}) async-start(bf16[256,8,2,512]{0,3,2,1:T(8,128)(2,1)} %bitcast.144), calls=%async_computation | async-start | bytes 8388608 | tf_op jit(solution)/shard_map/all_to_all | solution.py:153
  77.0 175.2 %all-gather.4.cloned.1.call-start = ((), (), s32[]{:S(2)}) async-start(), calls=%async_computation.5 | async-start | bytes 5242880 | tf_op jit(solution)/shard_map/all_gather | solution.py:11
  171.0 6.4 %copy-start.2 = (bf16[8,256,1,2,256]{4,1,0,3,2:T(8,128)(2,1)S(1)}, bf16[8,256,1,2,256]{4,1,0,3,2:T(8,128)(2,1)}, u32[]{:S(2)}) copy-start(bf16[8,256,1,2,256]{4,1,0,3,2:T(8,128)(2,1)} %copy.96) | copy-start | bytes 6291460
  183.2 11.6 %copy-start.1 = (bf16[256,4096]{1,0:T(8,128)(2,1)S(1)}, bf16[256,4096]{1,0:T(8,128)(2,1)}, u32[]{:S(2)}) copy-start(bf16[256,4096]{1,0:T(8,128)(2,1)} %param.11) | copy-start | bytes 6291460
  193.7 1.0 copy-start
  194.8 6.1 %copy-start.3 = (u32[32]{0:T(128)S(1)}, u32[32]{0:T(128)}, u32[]{:S(2)}) copy-start(u32[32]{0:T(128)} %constant.74) | copy-start | bytes 388
  197.3 52.6 %all-to-all-start.1 = ((bf16[256,8,2,256]{0,3,2,1:T(8,128)(2,1)}), bf16[256,8,2,256]{0,3,2,1:T(8,128)(2,1)S(1)}, u32[]{:S(2)}, u32[]{:S(2)}) async-start(bf16[256,8,2,256]{0,3,2,1:T(8,128)(2,1)} %bitcast.148), calls=%async_computation.1 | async-start | bytes 4194304 | tf_op jit(solution)/shard_map/all_to_all | solution.py:153
  300.5 98.6 %all-to-all-start.4 = ((bf16[2048,1,2,512]{3,2,1,0:T(2,128)(2,1)}), bf16[2048,1,2,512]{3,2,1,0:T(2,128)(2,1)}, u32[]{:S(2)}, u32[]{:S(2)}) async-start(bf16[2048,1,2,512]{3,2,1,0:T(2,128)(2,1)} %copy.109), calls=%async_computation.4 | async-start | bytes 8388608 | tf_op jit(solution)/shard_map/all_to_all | solution.py:96
Sparse Core Ops, SparseCore 0:
  194.9 51.5 all-gather.3
where the time goes:
time: 444 us; the launch traced here: 438 us
  waiting for transfers between devices  256 us (58%)
  local copies, waits for them, and re-layouts  74.7 us (17%)
  other arithmetic  35.6 us (8%)
  matrix products  24.3 us (5%)
  starting transfers between devices  22.9 us (5%)
  between operations  14.3 us (3%)
  blocking collectives  10.4 us (2%)
    all_to_all x4, waiting for transfers between devices, regroup_by_heads(): lax.all_to_all(as_sent(sending), 'head', split_axis=1, concat_axis=0, til...  168 us
    all_to_all x1, waiting for transfers between devices, send_back(): lax.all_to_all(retained[:, None], 'head', split_axis=0, concat_axis=1, ti...  87.4 us
    unnamed x16, local copies, waits for them, and re-layouts  21.2 us
    all_to_all x4, starting transfers between devices, regroup_by_heads(): lax.all_to_all(as_sent(sending), 'head', split_axis=1, concat_axis=0, til...  18.1 us
    dot_general x4, matrix products, emit_block(): jnp.einsum('nij,jnw->inw', weights, value_block, preferred_element_type=j...  11.7 us
    all_to_all x3, local copies, waits for them, and re-layouts, regroup_by_heads(): lax.all_to_all(as_sent(sending), 'head', split_axis=1, concat_axis=0, til...  11.1 us
    unnamed x1, blocking collectives  10.4 us
    another operation x1, local copies, waits for them, and re-layouts, send_back(): retained[:, None]  10.1 us
  transfers between devices with their start and end apart: 6, of which 5 were waited for; matrix products, arithmetic and copies ran while one was open for 7% of the time, Pallas kernels for 0%

commit v1 on v0

v1 whole, which is shorter than its diff:
```python
import functools

import jax
import jax.numpy as jnp
from jax import lax
from jax.experimental import pallas as pl
from jax.experimental.pallas import tpu as pltpu
from jax.sharding import PartitionSpec as P

MESH = pl.DeviceIdType.MESH
F32 = jnp.float32
BF16 = jnp.bfloat16
LAG = 2
CUTS = 2


def dot(a, b, dims):
    return lax.dot_general(a, b, (dims, ((), ())), preferred_element_type=F32)


def wide(column, times):
    return jnp.concatenate([column] * times, axis=1)


def retention_kernel(
    seqs, chips, heads, q_ref, k_ref, v_ref, dec_ref, out_ref,
    qbuf, kbuf, vbuf, decbuf, runcol, runrow, gath, coef, tri,
    abuf, ebuf, within, slow, retbuf, sbuf, rbuf, supb, rupb, sdnb, rdnb,
    xs, xr, loc, gs, gr, ss, sr, ups, upr, dns, dnr, rets, retr, retl,
):
    s = lax.axis_index("seq")
    h = lax.axis_index("head")
    c = lax.rem(h, 2)
    z = h // 2
    steps = seqs.bit_length() - 1
    rows = q_ref.shape[0]
    block = 2 * rows
    dk = qbuf.shape[2]
    dv = vbuf.shape[2]
    blocks = seqs * chips
    me = s * chips + z
    units = heads * CUTS
    urows = dk // CUTS
    mate = {"seq": s, "head": h + 1 - 2 * c}

    def spot(b):
        return {"seq": b // chips, "head": 2 * lax.rem(b, chips) + c}

    barrier = pltpu.get_barrier_semaphore()
    pl.semaphore_signal(barrier, inc=1, device_id=mate, device_id_type=MESH)

    def greet(o, _):
        pl.semaphore_signal(
            barrier, inc=1, device_id=spot(lax.rem(me + o, blocks)), device_id_type=MESH
        )
        return 0

    lax.fori_loop(1, blocks, greet, 0)
    pl.semaphore_wait(barrier, blocks)

    mine = pl.ds(pl.multiple_of(c * rows, rows), rows)

    def swap(kind, i):
        if kind == 3:
            source, target = dec_ref.at[1 - c], decbuf.at[mine]
        else:
            ref, buf = ((k_ref, kbuf), (v_ref, vbuf), (q_ref, qbuf))[kind]
            width = buf.shape[2]
            col = pl.multiple_of(((1 - c) * heads + i) * width, width)
            source, target = ref.at[:, pl.ds(col, width)], buf.at[i, mine, :]
        return pltpu.make_async_remote_copy(
            src_ref=source, dst_ref=target, send_sem=xs.at[kind, i], recv_sem=xr.at[kind, i],
            device_id=mate, device_id_type=MESH,
        )

    def keep(kind, i):
        if kind == 3:
            source, target = dec_ref.at[c], decbuf.at[mine]
        else:
            ref, buf = ((k_ref, kbuf), (v_ref, vbuf), (q_ref, qbuf))[kind]
            width = buf.shape[2]
            col = pl.multiple_of((c * heads + i) * width, width)
            source, target = ref.at[:, pl.ds(col, width)], buf.at[i, mine, :]
        return pltpu.make_async_copy(source, target, loc.at[kind, i])

    swap(3, 0).start()
    keep(3, 0).start()

    def launch(i, _):
        for kind in (0, 1):
            swap(kind, i).start()
            keep(kind, i).start()
        return 0

    lax.fori_loop(0, heads, launch, 0)

    def launch_q(i, _):
        swap(2, i).start()
        keep(2, i).start()
        return 0

    lax.fori_loop(0, heads, launch_q, 0)

    row_id = lax.broadcasted_iota(jnp.int32, (block, block), 0)
    col_id = lax.broadcasted_iota(jnp.int32, (block, block), 1)
    tri[...] = jnp.where(row_id >= col_id, 1.0, 0.0).astype(BF16)
    keep(3, 0).wait()
    swap(3, 0).wait_recv()
    dec = decbuf[...]
    running = dot(tri[...], dec, ((1,), (0,)))
    run_rows = dot(dec, tri[...], ((0,), (1,)))
    runrow[...] = run_rows[:heads, :][:, None, :]
    gath[me] = dot(dec, jnp.ones((block, dv), BF16), ((0,), (0,)))[:heads, :]
    for i in range(heads):
        runcol[i] = jnp.broadcast_to(running[:, i : i + 1], (block, 128))

    def tell(o, where):
        return pltpu.make_async_remote_copy(
            src_ref=gath.at[me], dst_ref=gath.at[where], send_sem=gs.at[o], recv_sem=gr.at[o],
            device_id=spot(lax.rem(me + o, blocks)), device_id_type=MESH,
        )

    def tell_start(o, _):
        tell(o, me).start()
        return 0

    lax.fori_loop(1, blocks, tell_start, 0)

    def hop(k, u):
        other = s ^ (1 << k)
        return pltpu.make_async_remote_copy(
            src_ref=sbuf.at[k, u], dst_ref=rbuf.at[k, u], send_sem=ss.at[k, u],
            recv_sem=sr.at[k, u], device_id={"seq": other, "head": h}, device_id_type=MESH,
        )

    def up(u):
        return pltpu.make_async_remote_copy(
            src_ref=supb.at[u], dst_ref=rupb.at[u], send_sem=ups.at[u], recv_sem=upr.at[u],
            device_id={"seq": s, "head": lax.rem(h + 2, 2 * chips)}, device_id_type=MESH,
        )

    def down(u):
        return pltpu.make_async_remote_copy(
            src_ref=sdnb.at[u], dst_ref=rdnb.at[u], send_sem=dns.at[u], recv_sem=dnr.at[u],
            device_id={"seq": s, "head": lax.rem(h - 2 + 2 * chips, 2 * chips)},
            device_id_type=MESH,
        )

    def bit(k):
        return lax.rem(s // (1 << k), 2)

    def sends(k):
        return True if k < steps - 1 else bit(k) == 0

    def gets(k):
        return True if k < steps - 1 else bit(k) == 1

    def state(i, _):
        for kind in (0, 1):
            keep(kind, i).wait()
            swap(kind, i).wait_recv()
        total = gath[me, pl.ds(i, 1), :][:, :128]
        fade = wide(jnp.exp(total - runcol[i]), dk // 128)
        faded = (kbuf[i].astype(F32) * fade).astype(BF16)
        for cut in range(CUTS):
            u = i * CUTS + cut
            part = dot(faded[:, cut * urows : (cut + 1) * urows], vbuf[i], ((0,), (0,)))
            abuf[u] = part
            if steps > 0:
                sbuf[0, u] = part.astype(BF16)

                @pl.when(sends(0))
                def _():
                    hop(0, u).start()

        return 0

    lax.fori_loop(0, heads, state, 0)

    def hear(o, _):
        tell(o, lax.rem(me - o + blocks, blocks)).wait_recv()
        return 0

    lax.fori_loop(1, blocks, hear, 0)

    def span(slot, lo, hi, live=None):
        total = lax.fori_loop(
            lo, hi, lambda b, acc: acc + gath[b], jnp.zeros((heads, dv), F32)
        )
        value = jnp.exp(total)
        if live is not None:
            value = value * live.astype(F32)
        coef[slot] = value

    def end(p, k):
        return p * chips + z + 1 if k == 0 else (p // (1 << k) + 1) * (1 << k) * chips

    for k in range(steps):
        other = s ^ (1 << k)
        span(3 * k, end(s, k), end(s, k + 1))
        span(3 * k + 1, end(other, k), end(s, k + 1))
        span(3 * k + 2, end(other, k), jnp.maximum(s * chips, end(other, k)), bit(k))
    base = 3 * steps
    span(base, me, me + 1)
    span(base + 1, s * chips, me + 1)
    span(base + 2, s * chips, me)

    @pl.when(z == 0)
    def _():
        rupb[...] = jnp.zeros(rupb.shape, BF16)

    @pl.when(z == chips - 1)
    def _():
        rdnb[...] = jnp.zeros(rdnb.shape, BF16)

    def scale(slot, u):
        return coef[slot, pl.ds(u // CUTS, 1), :]

    def when(live, u, fn):
        pl.when(jnp.logical_and(live, jnp.logical_and(u >= 0, u < units)))(lambda: fn(u))

    def step(t, _):
        for k in range(steps):

            def scan(u, k=k):
                @pl.when(gets(k))
                def _():
                    hop(k, u).wait_recv()
                    got = rbuf[k, u].astype(F32)
                    add = got * scale(3 * k + 2, u)
                    ebuf[u] = add if k == 0 else ebuf[u] + add
                    if k < steps - 1:
                        own = abuf[u] if k == 0 else sbuf[k, u].astype(F32)
                        sbuf[k + 1, u] = (
                            own * scale(3 * k, u) + got * scale(3 * k + 1, u)
                        ).astype(BF16)

                if k == 0 and steps == 1:

                    @pl.when(jnp.logical_not(gets(0)))
                    def _():
                        ebuf[u] = jnp.zeros((urows, dv), F32)

                if k < steps - 1:

                    @pl.when(sends(k + 1))
                    def _():
                        hop(k + 1, u).start()

            when(True, t - LAG * k, scan)
        if steps == 0:

            def blank(u):
                ebuf[u] = jnp.zeros((urows, dv), F32)

            when(True, t, blank)
        ready = t - LAG * max(steps - 1, 0)

        def rise(u):
            @pl.when(z > 0)
            def _():
                up(u).wait_recv()

            @pl.when(z < chips - 1)
            def _():
                supb[u] = (
                    rupb[u].astype(F32) * scale(base, u)
                    + abuf[u]
                    + scale(base + 1, u) * ebuf[u]
                ).astype(BF16)
                up(u).start()

        when(True, ready - LAG * z, rise)

        def sink(u):
            @pl.when(z < chips - 1)
            def _():
                down(u).wait_recv()

            @pl.when(z > 0)
            def _():
                sdnb[u] = (rdnb[u].astype(F32) + ebuf[u]).astype(BF16)
                down(u).start()

        when(True, ready - LAG * (chips - 1 - z), sink)

        def local(i):
            keep(2, i).wait()
            swap(2, i).wait_recv()
            scores = dot(qbuf[i], kbuf[i], ((1,), (1,)))
            spread = wide(runcol[i], block // 128) - runrow[i]
            row = lax.broadcasted_iota(jnp.int32, (block, block), 0)
            col = lax.broadcasted_iota(jnp.int32, (block, block), 1)
            factor = jnp.exp(jnp.where(row >= col, spread, -jnp.inf))
            weights = (scores * factor).astype(BF16)
            within[i] = dot(weights, vbuf[i], ((1,), (0,)))

        pl.when(t < heads)(lambda: local(t))

        def finish(u):
            i = u // CUTS
            start = rupb[u].astype(F32) + scale(base + 2, u) * (rdnb[u].astype(F32) + ebuf[u])
            slow[u] = start.astype(BF16)

            @pl.when(lax.rem(u, CUTS) == CUTS - 1)
            def _():
                low = slow[pl.ds(i * CUTS, CUTS)].reshape(dk, dv)
                across = dot(qbuf[i], low, ((1,), (0,)))
                across = across * wide(jnp.exp(runcol[i]), dv // 128)
                retbuf[i] = (within[i] + across).astype(BF16)
                give(i).start()
                stay(i).start()

        when(True, ready - LAG * jnp.maximum(z, chips - 1 - z), finish)
        return 0

    yours = pl.ds(pl.multiple_of((1 - c) * rows, rows), rows)

    def give(i):
        col = pl.multiple_of((c * heads + i) * dv, dv)
        return pltpu.make_async_remote_copy(
            src_ref=retbuf.at[i, yours, :], dst_ref=out_ref.at[:, pl.ds(col, dv)],
            send_sem=rets.at[i], recv_sem=retr.at[i], device_id=mate, device_id_type=MESH,
        )

    def take(i):
        col = pl.multiple_of(((1 - c) * heads + i) * dv, dv)
        return pltpu.make_async_remote_copy(
            src_ref=retbuf.at[i, yours, :], dst_ref=out_ref.at[:, pl.ds(col, dv)],
            send_sem=rets.at[i], recv_sem=retr.at[i], device_id=mate, device_id_type=MESH,
        )

    def stay(i):
        col = pl.multiple_of((c * heads + i) * dv, dv)
        return pltpu.make_async_copy(
            retbuf.at[i, mine, :], out_ref.at[:, pl.ds(col, dv)], retl.at[i]
        )

    total_steps = max(units + LAG * max(steps - 1, 0) + LAG * (chips - 1), heads)
    lax.fori_loop(0, total_steps, step, 0)

    swap(3, 0).wait_send()

    def close(i, _):
        for kind in range(3):
            swap(kind, i).wait_send()
        give(i).wait_send()
        take(i).wait_recv()
        stay(i).wait()
        return 0

    lax.fori_loop(0, heads, close, 0)

    def close_tell(o, _):
        tell(o, me).wait_send()
        return 0

    lax.fori_loop(1, blocks, close_tell, 0)

    def close_units(u, _):
        for k in range(steps):

            @pl.when(sends(k))
            def _():
                hop(k, u).wait_send()

        @pl.when(z < chips - 1)
        def _():
            up(u).wait_send()

        @pl.when(z > 0)
        def _():
            down(u).wait_send()

        return 0

    lax.fori_loop(0, units, close_units, 0)


def gate_kernel(ret_ref, gate_ref, out_ref):
    kept = ret_ref[...].astype(F32)
    centered = kept - jnp.mean(kept, axis=1, keepdims=True)
    variance = jnp.mean(centered * centered, axis=1, keepdims=True)
    normed = centered / jnp.sqrt(variance + 1e-06)
    gate = gate_ref[...].astype(F32)
    out_ref[...] = (jax.nn.silu(gate) * normed).astype(BF16)


def shards(seqs, groups, queries, key_vectors, values, decay_log, gate_input):
    rows, head_count = decay_log.shape
    heads = head_count // 2
    chips = groups // 2
    dk = queries.shape[1] // head_count
    dv = values.shape[1] // head_count
    block = 2 * rows
    blocks = seqs * chips
    units = heads * CUTS
    urows = dk // CUTS
    steps = seqs.bit_length() - 1
    hops = max(steps, 1)
    dec = jnp.pad(
        decay_log.reshape(rows, 2, heads).swapaxes(0, 1), ((0, 0), (0, 0), (0, 128 - heads))
    )
    hbm = pl.BlockSpec(memory_space=pl.ANY)
    dma = lambda *shape: pltpu.SemaphoreType.DMA(shape)
    retained = pl.pallas_call(
        functools.partial(retention_kernel, seqs, chips, heads),
        out_shape=jax.ShapeDtypeStruct(values.shape, BF16),
        in_specs=[hbm] * 4,
        out_specs=hbm,
        scratch_shapes=[
            pltpu.VMEM((heads, block, dk), BF16),
            pltpu.VMEM((heads, block, dk), BF16),
            pltpu.VMEM((heads, block, dv), BF16),
            pltpu.VMEM((block, 128), BF16),
            pltpu.VMEM((heads, block, 128), F32),
            pltpu.VMEM((heads, 1, block), F32),
            pltpu.VMEM((blocks, heads, dv), F32),
            pltpu.VMEM((3 * steps + 3, heads, dv), F32),
            pltpu.VMEM((block, block), BF16),
            pltpu.VMEM((units, urows, dv), F32),
            pltpu.VMEM((units, urows, dv), F32),
            pltpu.VMEM((heads, block, dv), F32),
            pltpu.VMEM((units, urows, dv), BF16),
            pltpu.VMEM((heads, block, dv), BF16),
            pltpu.VMEM((hops, units, urows, dv), BF16),
            pltpu.VMEM((hops, units, urows, dv), BF16),
            pltpu.VMEM((units, urows, dv), BF16),
            pltpu.VMEM((units, urows, dv), BF16),
            pltpu.VMEM((units, urows, dv), BF16),
            pltpu.VMEM((units, urows, dv), BF16),
            dma(4, heads), dma(4, heads), dma(4, heads),
            dma(blocks), dma(blocks),
            dma(hops, units), dma(hops, units),
            dma(units), dma(units), dma(units), dma(units),
            dma(heads), dma(heads), dma(heads),
        ],
        compiler_params=pltpu.CompilerParams(
            collective_id=0, has_side_effects=True, vmem_limit_bytes=67043328
        ),
    )(queries, key_vectors, values, dec)
    spec = pl.BlockSpec((rows, dv), lambda i: (0, i))
    return pl.pallas_call(
        gate_kernel,
        out_shape=jax.ShapeDtypeStruct(values.shape, BF16),
        grid=(head_count,),
        in_specs=[spec, spec],
        out_specs=spec,
    )(retained, gate_input)


def solution(mesh):
    spec = P(("seq", "head"), None)
    fn = functools.partial(shards, mesh.shape["seq"], mesh.shape["head"])
    return jax.shard_map(fn, mesh=mesh, in_specs=(spec,) * 5, out_specs=spec, check_vma=False)
```

time: 444 us -> 99.6 us (0.22); the launches traced: 438 us -> 99.1 us
  waiting for transfers between devices: 256 us -> 0 us
  Pallas kernels: 0 us -> 97.6 us
  local copies, waits for them, and re-layouts: 74.7 us -> 1.54 us
  other arithmetic: 35.6 us -> 0 us
  matrix products: 24.3 us -> 0 us
  starting transfers between devices: 22.9 us -> 0 us
  between operations: 14.3 us -> 0.02 us
  blocking collectives: 10.4 us -> 0 us
    all_to_all x5 -> x0, waiting for transfers between devices: 256 us -> none  [the longest x4 168 us: regroup_by_heads(): lax.all_to_all(as_sent(sending), 'head', split_axis=1, concat_axis=0, til...]
    pallas_call x0 -> x2, Pallas kernels: none -> 97.6 us  [the longest x1 84.4 us: shards(): pl.pallas_call(functools.partial(retention_kernel, seqs, chips, heads), o...]
    dot_general x9 -> x0, matrix products: 24.3 us -> none  [the longest x4 11.7 us: emit_block(): jnp.einsum('nij,jnw->inw', weights, value_block, preferred_element_type=j...]
    all_to_all x5 -> x0, starting transfers between devices: 22.9 us -> none  [the longest x4 18.1 us: regroup_by_heads(): lax.all_to_all(as_sent(sending), 'head', split_axis=1, concat_axis=0, til...]
    unnamed x16 -> x0, local copies, waits for them, and re-layouts: 21.2 us -> none
    convert_element_type x2 -> x0, local copies, waits for them, and re-layouts: 15.5 us -> none  [the longest x1 9.14 us: shards(): gathered_out.reshape(rows_here, head_count, value_width).astype(jnp.float32)]
    all_to_all x3 -> x0, local copies, waits for them, and re-layouts: 11.1 us -> none  [regroup_by_heads(): lax.all_to_all(as_sent(sending), 'head', split_axis=1, concat_axis=0, til...]
    unnamed x1 -> x0, blocking collectives: 10.4 us -> none
  transfers between devices with their start and end apart: 6 -> 0, of which waited for: 5 -> 0; matrix products, arithmetic and copies ran while one was open for 7% -> 0% of each run, Pallas kernels for 0% -> 0%
where the time goes in v1:
time: 99.6 us; the launch traced here: 99.1 us
  Pallas kernels  97.6 us (98%)
  local copies, waits for them, and re-layouts  1.54 us (2%)
    pallas_call x1, Pallas kernels, shards(): pl.pallas_call(functools.partial(retention_kernel, seqs, chips, heads), o...  84.4 us
    pallas_call x1, Pallas kernels, shards(): pl.pallas_call(gate_kernel, out_shape=jax.ShapeDtypeStruct(values.shape,...  13.2 us

profile of v1, /device:TPU:0, one launch (start us, length us, event | category | flops | bytes accessed | tf_op | source)
XLA Modules:
  0.0 99.1 jit_solution(1892238133948810688)
XLA Ops:
  0.0 0.9 copy.6
  0.9 0.7 pad.4.dec_ref
  1.5 84.4 %shard_map.55.ret_ref = bf16[256,8192]{1,0:T(8,128)(2,1)} custom-call(bf16[256,4096]{1,0:T(8,128)(2,1)} %q_ref.1, bf16[256,4096]{1,0:T(8,128)(2,1)} %k_ref.1, bf16[256,8192]{1,0:T(8,128)(2,1)} %v_ref.1, bf16[2,256,128]{2,1,0:T(8,128)(2,1)} %pad.4.dec_ref), custom_call_target="tpu_custom_call" | custom-call | tf_op jit(solution)/shard_map/pallas_call | solution.py:406
  85.9 13.2 %shard_map.56 = bf16[256,8192]{1,0:T(8,128)(2,1)} custom-call(bf16[256,8192]{1,0:T(8,128)(2,1)} %shard_map.55.ret_ref, bf16[256,8192]{1,0:T(8,128)(2,1)} %gate_ref.1), custom_call_target="tpu_custom_call" | custom-call | tf_op jit(solution)/shard_map/pallas_call | solution.py:443

commit v2 on v1

--- a/solution.py
+++ b/solution.py
@@ -10,8 +10,9 @@
 MESH = pl.DeviceIdType.MESH
 F32 = jnp.float32
 BF16 = jnp.bfloat16
-LAG = 2
-CUTS = 2
+LAG = 3
+CUTS = 4
+TILE = 64
 
 
 def dot(a, b, dims):
@@ -56,13 +57,11 @@
         return 0
 
     lax.fori_loop(1, blocks, greet, 0)
-    pl.semaphore_wait(barrier, blocks)
-
     mine = pl.ds(pl.multiple_of(c * rows, rows), rows)
 
     def swap(kind, i):
         if kind == 3:
-            source, target = dec_ref.at[1 - c], decbuf.at[mine]
+            source, target = dec_ref, decbuf.at[mine]
         else:
             ref, buf = ((k_ref, kbuf), (v_ref, vbuf), (q_ref, qbuf))[kind]
             width = buf.shape[2]
@@ -74,25 +73,31 @@
         )
 
     def keep(kind, i):
-        if kind == 3:
-            source, target = dec_ref.at[c], decbuf.at[mine]
-        else:
-            ref, buf = ((k_ref, kbuf), (v_ref, vbuf), (q_ref, qbuf))[kind]
-            width = buf.shape[2]
-            col = pl.multiple_of((c * heads + i) * width, width)
-            source, target = ref.at[:, pl.ds(col, width)], buf.at[i, mine, :]
+        ref, buf = ((k_ref, kbuf), (v_ref, vbuf), (q_ref, qbuf))[kind]
+        width = buf.shape[2]
+        col = pl.multiple_of((c * heads + i) * width, width)
+        source, target = ref.at[:, pl.ds(col, width)], buf.at[i, mine, :]
         return pltpu.make_async_copy(source, target, loc.at[kind, i])
-
-    swap(3, 0).start()
-    keep(3, 0).start()
 
     def launch(i, _):
         for kind in (0, 1):
+            keep(kind, i).start()
+        return 0
+
+    lax.fori_loop(0, heads, launch, 0)
+    row_id = lax.broadcasted_iota(jnp.int32, (block, block), 0)
+    col_id = lax.broadcasted_iota(jnp.int32, (block, block), 1)
+    tri[...] = jnp.where(row_id >= col_id, 1.0, 0.0).astype(BF16)
+    decbuf[mine] = dec_ref[...]
+    pl.semaphore_wait(barrier, blocks)
+    swap(3, 0).start()
+
+    def launch_swap(i, _):
+        for kind in (0, 1):
             swap(kind, i).start()
-            keep(kind, i).start()
-        return 0
-
-    lax.fori_loop(0, heads, launch, 0)
+        return 0
+
+    lax.fori_loop(0, heads, launch_swap, 0)
 
     def launch_q(i, _):
         swap(2, i).start()
@@ -100,17 +105,15 @@
         return 0
 
     lax.fori_loop(0, heads, launch_q, 0)
-
-    row_id = lax.broadcasted_iota(jnp.int32, (block, block), 0)
-    col_id = lax.broadcasted_iota(jnp.int32, (block, block), 1)
-    tri[...] = jnp.where(row_id >= col_id, 1.0, 0.0).astype(BF16)
-    keep(3, 0).wait()
     swap(3, 0).wait_recv()
     dec = decbuf[...]
     running = dot(tri[...], dec, ((1,), (0,)))
     run_rows = dot(dec, tri[...], ((0,), (1,)))
-    runrow[...] = run_rows[:heads, :][:, None, :]
-    gath[me] = dot(dec, jnp.ones((block, dv), BF16), ((0,), (0,)))[:heads, :]
+    running = jnp.where(c == 0, running[:, :heads], running[:, heads:])
+    run_rows = jnp.where(c == 0, run_rows[:heads, :], run_rows[heads:, :])
+    totals = dot(dec, jnp.ones((block, dv), BF16), ((0,), (0,)))
+    gath[me] = jnp.where(c == 0, totals[:heads, :], totals[heads:, :])
+    runrow[...] = run_rows[:, None, :]
     for i in range(heads):
         runcol[i] = jnp.broadcast_to(running[:, i : i + 1], (block, 128))
 
@@ -295,7 +298,7 @@
             weights = (scores * factor).astype(BF16)
             within[i] = dot(weights, vbuf[i], ((1,), (0,)))
 
-        pl.when(t < heads)(lambda: local(t))
+        pl.when(jnp.logical_and(lax.rem(t, CUTS) == 0, t < units))(lambda: local(t // CUTS))
 
         def finish(u):
             i = u // CUTS
@@ -336,7 +339,7 @@
             retbuf.at[i, mine, :], out_ref.at[:, pl.ds(col, dv)], retl.at[i]
         )
 
-    total_steps = max(units + LAG * max(steps - 1, 0) + LAG * (chips - 1), heads)
+    total_steps = units + LAG * max(steps - 1, 0) + LAG * (chips - 1)
     lax.fori_loop(0, total_steps, step, 0)
 
     swap(3, 0).wait_send()
@@ -377,13 +380,17 @@
     lax.fori_loop(0, units, close_units, 0)
 
 
-def gate_kernel(ret_ref, gate_ref, out_ref):
-    kept = ret_ref[...].astype(F32)
-    centered = kept - jnp.mean(kept, axis=1, keepdims=True)
-    variance = jnp.mean(centered * centered, axis=1, keepdims=True)
-    normed = centered / jnp.sqrt(variance + 1e-06)
-    gate = gate_ref[...].astype(F32)
-    out_ref[...] = (jax.nn.silu(gate) * normed).astype(BF16)
+def gate_kernel(heads, ret_ref, gate_ref, out_ref):
+    width = ret_ref.shape[1] // heads
+    for i in range(heads):
+        part = pl.ds(i * width, width)
+        kept = ret_ref[:, part].astype(F32)
+        centered = kept - jnp.mean(kept, axis=1, keepdims=True)
+        variance = jnp.mean(centered * centered, axis=1, keepdims=True)
+        gate = gate_ref[:, part].astype(F32)
+        half = 0.5 * gate
+        swish = half + half * jnp.tanh(half)
+        out_ref[:, part] = (swish * (centered * lax.rsqrt(variance + 1e-06))).astype(BF16)
 
 
 def shards(seqs, groups, queries, key_vectors, values, decay_log, gate_input):
@@ -398,21 +405,18 @@
     urows = dk // CUTS
     steps = seqs.bit_length() - 1
     hops = max(steps, 1)
-    dec = jnp.pad(
-        decay_log.reshape(rows, 2, heads).swapaxes(0, 1), ((0, 0), (0, 0), (0, 128 - heads))
-    )
     hbm = pl.BlockSpec(memory_space=pl.ANY)
     dma = lambda *shape: pltpu.SemaphoreType.DMA(shape)
     retained = pl.pallas_call(
         functools.partial(retention_kernel, seqs, chips, heads),
         out_shape=jax.ShapeDtypeStruct(values.shape, BF16),
-        in_specs=[hbm] * 4,
+        in_specs=[hbm] * 3 + [pl.BlockSpec(memory_space=pltpu.VMEM)],
         out_specs=hbm,
         scratch_shapes=[
             pltpu.VMEM((heads, block, dk), BF16),
             pltpu.VMEM((heads, block, dk), BF16),
             pltpu.VMEM((heads, block, dv), BF16),
-            pltpu.VMEM((block, 128), BF16),
+            pltpu.VMEM((block, head_count), BF16),
             pltpu.VMEM((heads, block, 128), F32),
             pltpu.VMEM((heads, 1, block), F32),
             pltpu.VMEM((blocks, heads, dv), F32),
@@ -438,12 +442,13 @@
         compiler_params=pltpu.CompilerParams(
             collective_id=0, has_side_effects=True, vmem_limit_bytes=67043328
         ),
-    )(queries, key_vectors, values, dec)
-    spec = pl.BlockSpec((rows, dv), lambda i: (0, i))
+    )(queries, key_vectors, values, decay_log)
+    tile = min(TILE, rows)
+    spec = pl.BlockSpec((tile, values.shape[1]), lambda i: (i, 0))
     return pl.pallas_call(
-        gate_kernel,
+        functools.partial(gate_kernel, head_count),
         out_shape=jax.ShapeDtypeStruct(values.shape, BF16),
-        grid=(head_count,),
+        grid=(rows // tile,),
         in_specs=[spec, spec],
         out_specs=spec,
     )(retained, gate_input)

time: 99.6 us -> 90.8 us (0.912)
  Pallas kernels: 97.6 us -> 89.1 us
    pallas_call x1, Pallas kernels: 13.2 us -> 8.29 us  [shards(): pl.pallas_call(functools.partial(gate_kernel, head_count), out_shape=jax....]
    pallas_call x1, Pallas kernels: 84.4 us -> 80.8 us  [shards(): pl.pallas_call(functools.partial(retention_kernel, seqs, chips, heads), o...]
    unnamed x0 -> x1, local copies, waits for them, and re-layouts: none -> 1.43 us
where the time goes in v2:
time: 90.8 us; the launch traced here: 90.5 us
  Pallas kernels  89.1 us (98%)
  local copies, waits for them, and re-layouts  1.43 us (2%)
    pallas_call x1, Pallas kernels, shards(): pl.pallas_call(functools.partial(retention_kernel, seqs, chips, heads), o...  80.8 us
    pallas_call x1, Pallas kernels, shards(): pl.pallas_call(functools.partial(gate_kernel, head_count), out_shape=jax....  8.29 us

profile of v2, /device:TPU:0, one launch (start us, length us, event | category | flops | bytes accessed | tf_op | source)
XLA Modules:
  0.0 90.5 jit_solution(13265798711682982507)
XLA Ops:
  0.0 1.4 %copy.6.dec_ref = bf16[256,16]{1,0:T(8,128)(2,1)} copy(bf16[256,16]{0,1:T(8,128)(2,1)} %param.8) | data formatting | bytes 16384 | tf_op args[3]
  1.4 80.8 %shard_map.55.ret_ref = bf16[256,8192]{1,0:T(8,128)(2,1)} custom-call(bf16[256,4096]{1,0:T(8,128)(2,1)} %q_ref.1, bf16[256,4096]{1,0:T(8,128)(2,1)} %k_ref.1, bf16[256,8192]{1,0:T(8,128)(2,1)} %v_ref.1, bf16[256,16]{1,0:T(8,128)(2,1)} %copy.6.dec_ref), custom_call_target="tpu_custom_call" | custom-call | tf_op jit(solution)/shard_map/pallas_call | solution.py:410
  82.2 8.3 %shard_map.56 = bf16[256,8192]{1,0:T(8,128)(2,1)} custom-call(bf16[256,8192]{1,0:T(8,128)(2,1)} %shard_map.55.ret_ref, bf16[256,8192]{1,0:T(8,128)(2,1)} %gate_ref.1), custom_call_target="tpu_custom_call" | custom-call | tf_op jit(solution)/shard_map/pallas_call | solution.py:448
